TPU v7x, 128 devices: a whole 4x4x4 slice. The times are simulated.
128 devices in a mesh: dp: 1, tp: 2 (over core), sp: 64 (over z, y, x).
Axes of the slice: x: 4, y: 4, z: 4, core: 2. Of those that a mesh axis runs over, the one named last changes fastest.
Arguments:
- hidden: bfloat16 [32, 5120], P('dp')
- lat_cache: bfloat16 [32, 16384, 512], P('dp', 'sp')
- rope_cache: bfloat16 [32, 16384, 64], P('dp', 'sp')
- positions: int32 [32], P('dp')
- w_dq: bfloat16 [5120, 1536], replicated
- gain_q: bfloat16 [1536], replicated
- w_dkv: bfloat16 [5120, 576], replicated
- gain_kv: bfloat16 [512], replicated
- w_uq: bfloat16 [1536, 128, 192], P(None, 'tp')
- w_uk: bfloat16 [512, 128, 128], P(None, 'tp')
- w_uv: bfloat16 [512, 128, 128], P(None, 'tp')
- w_out: bfloat16 [16384, 5120], P('tp')
Outputs:
- output 1: bfloat16 [32, 5120], P('dp')
- output 2: bfloat16 [32, 16384, 512], P('dp', 'sp')
- output 3: bfloat16 [32, 16384, 64], P('dp', 'sp')
All inputs are finite; a program needn't handle non-finite values.
Results may differ from a plain program's by a relative error of at most 0.00918123.
Values sent between devices are 32-bit elements.
A program may use at most 1 GiB of HBM per device.

v0:
```python
import math
import jax
import jax.numpy as jnp
from jax import lax
from jax.sharding import PartitionSpec as P

EPSILON = 1e-6
ROPE_BASE = 50000.0
YARN_MSCALE = 1.0 + 0.1 * math.log(32.0)
MASK_VALUE = -1e30


def rms_norm(values, gain):
    vals32 = values.astype(jnp.float32)
    inv_rms = lax.rsqrt(jnp.mean(vals32 * vals32, axis=-1, keepdims=True) + EPSILON)
    return vals32 * inv_rms * gain.astype(jnp.float32)


def rope_tables(positions, rope_dim):
    half_dim = rope_dim // 2
    inv_freq = ROPE_BASE ** (-jnp.arange(half_dim).astype(jnp.float32) / half_dim)
    angles = positions.astype(jnp.float32)[:, None] * inv_freq[None, :]
    return jnp.cos(angles), jnp.sin(angles)


def rotate_pairs(values, cos_t, sin_t):
    half_dim = values.shape[-1] // 2
    first_half = values[..., :half_dim]
    second_half = values[..., half_dim:]
    return jnp.concatenate([first_half * cos_t - second_half * sin_t, second_half * cos_t + first_half * sin_t], axis=-1)


def project_inputs(hidden, positions, w_dq, gain_q, w_dkv, gain_kv, w_uq, w_uk):
    kv_rank = w_uk.shape[0]
    nope_dim = w_uk.shape[2]
    cos_t, sin_t = rope_tables(positions, w_uq.shape[2] - nope_dim)
    h_q = jnp.dot(hidden, w_dq, preferred_element_type=jnp.float32).astype(jnp.bfloat16)
    c_q = rms_norm(h_q, gain_q).astype(jnp.bfloat16)
    q_full = jnp.einsum('br,rhd->bhd', c_q, w_uq, preferred_element_type=jnp.float32).astype(jnp.bfloat16)
    q_rope = rotate_pairs(q_full[:, :, nope_dim:].astype(jnp.float32), cos_t[:, None, :], sin_t[:, None, :]).astype(jnp.bfloat16)
    q_abs = jnp.einsum('bhn,khn->bhk', q_full[:, :, :nope_dim], w_uk, preferred_element_type=jnp.float32).astype(jnp.bfloat16)
    kv_down = jnp.dot(hidden, w_dkv, preferred_element_type=jnp.float32).astype(jnp.bfloat16)
    lat_new = rms_norm(kv_down[:, :kv_rank], gain_kv).astype(jnp.bfloat16)
    rope_new = rotate_pairs(kv_down[:, kv_rank:].astype(jnp.float32), cos_t, sin_t).astype(jnp.bfloat16)
    return q_abs, q_rope, lat_new, rope_new


def solution(mesh):
    row_spec = P('dp', None)
    cache_spec = P('dp', 'sp', None)
    head_spec = P(None, 'tp', None)
    in_specs = (row_spec, cache_spec, cache_spec, P('dp'), P(), P(), P(), P(), head_spec, head_spec, head_spec, P('tp', None))
    out_specs = (row_spec, cache_spec, cache_spec)

    def local_step(hidden, lat_cache, rope_cache, positions, w_dq, gain_q, w_dkv, gain_kv, w_uq, w_uk, w_uv, w_out):
        rows_local = hidden.shape[0]
        seq_local = lat_cache.shape[1]
        score_scale = YARN_MSCALE ** 2 / math.sqrt(w_uq.shape[2])
        q_abs, q_rope, lat_new, rope_new = project_inputs(hidden, positions, w_dq, gain_q, w_dkv, gain_kv, w_uq, w_uk)
        slot_ids = lax.axis_index('sp') * seq_local + jnp.arange(seq_local)
        slot_hit = (slot_ids[None, :] == positions[:, None])[:, :, None]
        lat_all = jnp.where(slot_hit, lat_new[:, None, :], lat_cache)
        rope_all = jnp.where(slot_hit, rope_new[:, None, :], rope_cache)
        scores = (jnp.einsum('bhk,bsk->bhs', q_abs, lat_all, preferred_element_type=jnp.float32) + jnp.einsum('bhr,bsr->bhs', q_rope, rope_all, preferred_element_type=jnp.float32)) * score_scale
        key_valid = slot_ids[None, None, :] <= positions[:, None, None]
        scores = jnp.where(key_valid, scores, MASK_VALUE)
        max_global = lax.pmax(jnp.max(scores, axis=-1), 'sp')
        weights = jnp.exp(scores - max_global[:, :, None])
        lat_part = jnp.einsum('bhs,bsk->bhk', weights.astype(jnp.bfloat16), lat_all, preferred_element_type=jnp.float32)
        denominator, lat_sum = lax.psum((jnp.sum(weights, axis=-1), lat_part), 'sp')
        o_lat = (lat_sum / denominator[:, :, None]).astype(jnp.bfloat16)
        o_heads = jnp.einsum('bhk,khv->bhv', o_lat, w_uv, preferred_element_type=jnp.float32).astype(jnp.bfloat16)
        attn_part = jnp.dot(o_heads.reshape(rows_local, -1), w_out, preferred_element_type=jnp.float32)
        attn_out = lax.psum(attn_part, 'tp')
        return (hidden.astype(jnp.float32) + attn_out).astype(jnp.bfloat16), lat_all, rope_all

    return jax.shard_map(local_step, mesh=mesh, in_specs=in_specs, out_specs=out_specs, check_vma=False)
```

profile of v0, /device:TPU:1, one launch (start us, length us, event | category | flops | bytes accessed | tf_op | source)
XLA Modules:
  0.0 854.1 jit_solution(1949833244315950489)
XLA Ops:
  7.2 0.0 all-reduce.3.cloned.1.call-start
  7.3 4.6 convolution_convert_fusion.2
  11.9 0.1 fusion.37
  12.1 0.1 broadcast_compare_fusion.1
  12.2 8.3 multiply_reduce_fusion
  20.5 17.8 %convolution_convert_fusion.1 = bf16[32,64,192]{2,0,1:T(8,128)(2,1)S(1)} fusion(bf16[1536,64,192]{0,2,1:T(8,128)(2,1)} %param.20, f32[32,1536]{1,0:T(8,128)S(1)} %get-tuple-element.14, f32[1536]{0:T(1024)S(1)} %convert_element_type.76, f32[32]{0:T(128)S(1)} %add_rsqrt_fusion.1), kind=kOutput, calls=%fused_computation.16 | convolution fusion | flops 1208500224 | bytes 38738048 | tf_op jit(solution)/shard_map/br,rhd->bhd/dot_general | solution.py:39
  38.3 1.0 copy-done.2
  39.3 0.1 slice_convert_fusion
  39.4 22.4 %convert_bitcast_fusion = bf16[32,64,512]{2,0,1:T(8,128)(2,1)} fusion(bf16[512,64,128]{2,1,0:T(8,128)(2,1)} %param.21, bf16[32,64,192]{2,0,1:T(8,128)(2,1)} %copy-done.2), kind=kOutput, calls=%fused_computation.13 | convolution fusion | flops 269484032 | bytes 11010048 | tf_op jit(solution)/shard_map/bhn,khn->bhk/dot_general | solution.py:41
  61.8 0.1 fusion.39
  61.9 0.1 multiply_cosine_fusion
  62.0 0.1 pad_maximum_fusion.1
  62.1 0.4 subtract_convert_fusion
  62.6 0.3 pad_maximum_fusion
  62.9 0.2 copy-done.4
  63.0 0.3 broadcast_select_fusion.1
  63.4 1.0 copy-done.1
  64.4 0.4 fusion.31
  64.8 1.4 broadcast_select_fusion
  66.3 5.9 fusion.40
  72.2 296.4 %pmax.7 = f32[32,64]{1,0:T(8,128)S(1)} all-reduce(f32[32,64]{1,0:T(8,128)S(1)} %get-tuple-element.15), channel_id=1, replica_groups=mesh['dp'=1,'tp'=2,'sp'=64] {'sp'}, use_global_device_ids=true, to_apply=%region_3.4 | all-reduce | flops 2048 | bytes 16384 | tf_op jit(solution)/shard_map/pmax | solution.py:67
  368.6 6.8 fusion.24
  375.4 0.0 all-reduce.3.cloned.1.call-update
  375.4 0.0 all-reduce.5.cloned.1.call-start
  375.5 0.6 fusion.10
  376.1 287.2 %psum.22 = f32[32,64]{1,0:T(8,128)S(1)} all-reduce(f32[32,64]{1,0:T(8,128)S(1)} %fusion.10), channel_id=1, replica_groups=mesh['dp'=1,'tp'=2,'sp'=64] {'sp'}, use_global_device_ids=true, to_apply=%region_6.7 | all-reduce | flops 2048 | bytes 16384 | tf_op jit(solution)/shard_map/psum | solution.py:70
  663.4 0.0 all-reduce.3.cloned.1.call-done
  663.4 2.6 divide_convert_fusion
  666.0 21.9 %fusion.19 = bf16[64,4,8,128]{3,2,1,0:T(8,128)(2,1)S(1)} fusion(bf16[512,64,128]{2,1,0:T(8,128)(2,1)} %param.22, bf16[32,64,512]{2,1,0:T(8,128)(2,1)S(1)} %divide_convert_fusion), kind=kOutput, calls=%fused_computation.18 | convolution fusion | flops 268697600 | bytes 11010048 | tf_op jit(solution)/shard_map/bhk,khv->bhv/dot_general | solution.py:72
  687.9 29.7 %fusion.27 = f32[32,5120]{1,0:T(8,128)} fusion(bf16[8192,5120]{1,0:T(8,128)(2,1)} %param.23, bf16[64,4,8,128]{3,2,1,0:T(8,128)(2,1)S(1)} %fusion.19), kind=kOutput, calls=%fused_computation.26 | convolution fusion | flops 2684354560 | bytes 85065728 | tf_op jit(solution)/shard_map/dot_general | solution.py:73
  717.6 127.5 %all-reduce.5.cloned.1.call-done = f32[32,5120]{1,0:T(8,128)} async-done(((f32[32,5120]{1,0:T(8,128)}), f32[32,5120]{1,0:T(8,128)}) %all-reduce.5.cloned.1.call-update) | async-done | bytes 655376 | tf_op jit(solution)/shard_map/psum | solution.py:74
  845.1 1.9 add_convert_fusion.1
  (27 shorter events, 0.1 us)
Async XLA Ops:
  7.2 5.0 copy-start.3
  7.2 4.8 copy-start.7
  7.2 4.9 copy-start.6
  7.2 4.9 copy-start.5
  7.2 656.2 %all-reduce.3.cloned.1.call-start = ((), (), s32[]{:S(2)}) async-start(), calls=%async_computation | async-start | bytes 8388608 | tf_op jit(solution)/shard_map/psum | solution.py:70
  38.3 1.0 copy-start.2
  39.3 25.5 %slice-start = ((s8[8388608]{0:T(1024)(128)(4,1)}), s8[4194304]{0:T(1024)(128)(4,1)S(1)}, s32[]{:S(2)}) async-start(s8[8388608]{0:T(1024)(128)(4,1)} %bitcast.20), calls=%async_computation.2 | async-start | bytes 8388608
  39.4 25.4 %slice-start.1 = ((s8[8388608]{0:T(1024)(128)(4,1)}), s8[4194304]{0:T(1024)(128)(4,1)S(1)}, s32[]{:S(2)}) async-start(s8[8388608]{0:T(1024)(128)(4,1)} %bitcast.20), calls=%async_computation.3 | async-start | bytes 8388608
  61.8 1.2 copy-start.4
  63.4 1.0 copy-start.1
  66.2 6.0 copy-start
  375.4 469.7 %all-reduce.5.cloned.1.call-start = ((), (), s32[]{:S(2)}) async-start(), calls=%async_computation.1 | async-start | bytes 1310720 | tf_op jit(solution)/shard_map/psum | solution.py:74
Sparse Core Ops, SparseCore 0:
  375.6 185.8 all-reduce.2
  717.8 127.3 all-reduce.4
where the time goes:
time: 859 us; the launch traced here: 854 us
  blocking collectives  584 us (68%)
  waiting for transfers between devices  128 us (15%)
  matrix products  118 us (14%)
  between operations  14.5 us (2%)
    pmax x1, blocking collectives, local_step(): max_global = lax.pmax(jnp.max(scores, axis=-1), 'sp')  296 us
    psum x1, blocking collectives, local_step(): denominator, lat_sum = lax.psum((jnp.sum(weights, axis=-1), lat_part), 'sp')  287 us
    psum x1, waiting for transfers between devices, local_step(): attn_out = lax.psum(attn_part, 'tp')  127 us
    dot_general x1, matrix products, local_step(): jnp.dot(o_heads.reshape(rows_local, -1), w_out, preferred_element_type=jn...  29.7 us
    dot_general x1, matrix products, project_inputs(): jnp.einsum('bhn,khn->bhk', q_full[:, :, :nope_dim], w_uk, preferred_eleme...  22.4 us
    dot_general x1, matrix products, local_step(): jnp.einsum('bhk,khv->bhv', o_lat, w_uv, preferred_element_type=jnp.float32)  21.9 us
    dot_general x1, matrix products, project_inputs(): jnp.einsum('br,rhd->bhd', c_q, w_uq, preferred_element_type=jnp.float32)  17.8 us
  transfers between devices with their start and end apart: 2, of which 1 were waited for; matrix products, arithmetic and copies ran while one was open for 0% of the time, Pallas kernels for 0%

commit v1 on v0

--- a/solution.py
+++ b/solution.py
@@ -2,12 +2,23 @@
 import jax
 import jax.numpy as jnp
 from jax import lax
+from jax.experimental import pallas as pl
+from jax.experimental.pallas import tpu as pltpu
 from jax.sharding import PartitionSpec as P
 
 EPSILON = 1e-6
 ROPE_BASE = 50000.0
 YARN_MSCALE = 1.0 + 0.1 * math.log(32.0)
 MASK_VALUE = -1e30
+MESH = pl.DeviceIdType.MESH
+
+HEAD_STRIDE = (16, 4, 1)
+SP_STRIDE = (1, 4, 16)
+ORDERS = ((0, 1, 2), (1, 2, 0), (2, 0, 1))
+UNIT_LO = (0, 5, 10)
+UNIT_HI = (5, 10, 16)
+OUT_LO = (0, 256)
+OUT_HI = (256, 640)
 
 
 def rms_norm(values, gain):
@@ -45,6 +56,278 @@
     return q_abs, q_rope, lat_new, rope_new
 
 
+def tail_kernel(u_ref, st_ref, hid_ref, wuv_ref, wout_ref, out_ref,
+                r1, v1, r2, v2, r3, s1, s2, q1, q2, q3,
+                wuv_v, wuv_h, wout_v, y_buf, y_in, t1, t2, p1, p2, zbuf, g_buf,
+                send_sem, recv_sem, load_sem):
+    sp = lax.axis_index('sp')
+    tp = lax.axis_index('tp')
+    coord = (lax.rem(sp, 4), lax.rem(sp // 4, 4), sp // 16)
+    head = coord[0] * 16 + coord[1] * 4 + coord[2]
+    group = pl.multiple_of((head // 8) * 8, 8)
+
+    load_uv = pltpu.make_async_copy(wuv_ref.at[:, pl.ds(group, 8), :], wuv_v, load_sem.at[0])
+    load_uv.start()
+    load_out = pltpu.make_async_copy(wout_ref.at[pl.ds(pl.multiple_of(head * 128, 128), 128), :], wout_v, load_sem.at[1])
+    load_out.start()
+
+    def peer_coord(axis, step):
+        return lax.rem(coord[axis] + step, 4)
+
+    def peer_id(axis, step):
+        return {'sp': sp + (peer_coord(axis, step) - coord[axis]) * SP_STRIDE[axis]}
+
+    barrier = pltpu.get_barrier_semaphore()
+    for axis in range(3):
+        for step in range(1, 4):
+            pl.semaphore_signal(barrier, inc=1, device_id=peer_id(axis, step), device_id_type=MESH)
+    pl.semaphore_signal(barrier, inc=1, device_id={'tp': 1 - tp}, device_id_type=MESH)
+    pl.semaphore_wait(barrier, 10)
+
+    started = []
+
+    def send(src, dst, device):
+        index = len(started)
+        copy = pltpu.make_async_remote_copy(
+            src_ref=src, dst_ref=dst, send_sem=send_sem.at[index], recv_sem=recv_sem.at[index],
+            device_id=device, device_id_type=MESH)
+        copy.start()
+        started.append(copy)
+        return copy
+
+    lane = lax.broadcasted_iota(jnp.int32, (2, 8, 128), 2)
+
+    def merge_stats(stats, offset):
+        top = jnp.maximum(jnp.maximum(stats[0], stats[1]), jnp.maximum(stats[2], stats[3]))
+        shift = lax.rem(128 - offset, 128)
+        factors = [jnp.exp(s - top) for s in stats]
+        den = sum(f * pltpu.roll(s, 64, 2) for f, s in zip(factors, stats))
+        merged = jnp.where(lane < 64, top, pltpu.roll(den, 64, 2))
+        return pltpu.roll(merged, shift, 2), [pltpu.roll(f, shift, 2) for f in factors]
+
+    def spread(factor, lane_index):
+        return jnp.broadcast_to(factor[:, lane_index:lane_index + 1], (8, 128))
+
+    pending = {}
+    for colour in range(3):
+        axis = ORDERS[colour][0]
+        lo, hi = UNIT_LO[colour], UNIT_HI[colour]
+        for step in (2, 1, 3):
+            pc = peer_coord(axis, step)
+            sel = [slice(None)] * 3
+            sel[axis] = pc
+            src = u_ref.at[(pl.ds(lo, hi - lo),) + tuple(sel)]
+            a = send(src, r1.at[step - 1, pl.ds(lo, hi - lo)], peer_id(axis, step))
+            b = send(st_ref.at[pl.ds(colour, 2)], q1.at[colour, step - 1], peer_id(axis, step))
+            pending[colour, step] = (a, b)
+
+    load_uv.wait()
+    pick = lax.broadcasted_iota(jnp.int32, (64, 8, 128), 1) == lax.rem(head, 8)
+
+    def pick_rows(i, carry):
+        rows = pl.ds(pl.multiple_of(i * 64, 64), 64)
+        block = wuv_v[rows].astype(jnp.float32)
+        wuv_h[rows, :] = jnp.sum(jnp.where(pick, block, 0.0), axis=1).astype(jnp.bfloat16)
+        return carry
+
+    lax.fori_loop(0, 8, pick_rows, 0)
+
+    for colour in range(3):
+        order = ORDERS[colour]
+        axis = order[0]
+        lo, hi = UNIT_LO[colour], UNIT_HI[colour]
+        for step in (1, 3, 2):
+            for copy in pending[colour, step]:
+                copy.wait_recv()
+        stats = [st_ref[pl.ds(colour, 2)]] + [q1[colour, i] for i in range(3)]
+        merged, factors = merge_stats(stats, coord[axis] * HEAD_STRIDE[axis])
+        s1[colour] = merged
+        first, second = [a for a in range(3) if a != axis]
+        own = [slice(None)] * 3
+        own[axis] = coord[axis]
+        for i in range(4):
+            for j in range(4):
+                where = HEAD_STRIDE[first] * i + HEAD_STRIDE[second] * j
+                at = [None] * 3
+                at[axis], at[first], at[second] = coord[axis], i, j
+                for bt in range(lo // 4, (hi - 1) // 4 + 1):
+                    fb = [spread(f[bt - colour], where) for f in factors]
+                    for unit in range(max(lo, bt * 4), min(hi, bt * 4 + 4)):
+                        total = fb[0] * u_ref[unit, at[0], at[1], at[2]]
+                        for k in range(3):
+                            total = total + fb[k + 1] * r1[k, unit, i, j]
+                        v1[unit, i, j] = total
+        axis2 = order[1]
+        for step in (2, 1, 3):
+            pc = peer_coord(axis2, step)
+            sel = (pc, slice(None)) if axis2 == first else (slice(None), pc)
+            a = send(v1.at[(pl.ds(lo, hi - lo),) + sel], r2.at[step - 1, pl.ds(lo, hi - lo)], peer_id(axis2, step))
+            b = send(s1.at[colour], q2.at[colour, step - 1], peer_id(axis2, step))
+            pending[colour, step] = (a, b)
+
+    for colour in range(3):
+        order = ORDERS[colour]
+        axis, axis2, axis3 = order
+        lo, hi = UNIT_LO[colour], UNIT_HI[colour]
+        first, second = [a for a in range(3) if a != axis]
+        for step in (1, 3, 2):
+            for copy in pending[colour, step]:
+                copy.wait_recv()
+        stats = [s1[colour]] + [q2[colour, i] for i in range(3)]
+        merged, factors = merge_stats(stats, coord[axis2] * HEAD_STRIDE[axis2])
+        s2[colour] = merged
+        for i in range(4):
+            at = (coord[axis2], i) if axis2 == first else (i, coord[axis2])
+            for bt in range(lo // 4, (hi - 1) // 4 + 1):
+                fb = [spread(f[bt - colour], HEAD_STRIDE[axis3] * i) for f in factors]
+                for unit in range(max(lo, bt * 4), min(hi, bt * 4 + 4)):
+                    total = fb[0] * v1[unit, at[0], at[1]]
+                    for k in range(3):
+                        total = total + fb[k + 1] * r2[k, unit, i]
+                    v2[unit, i] = total
+        for step in (2, 1, 3):
+            a = send(v2.at[pl.ds(lo, hi - lo), peer_coord(axis3, step)], r3.at[step - 1, pl.ds(lo, hi - lo)], peer_id(axis3, step))
+            b = send(s2.at[colour], q3.at[colour, step - 1], peer_id(axis3, step))
+            pending[colour, step] = (a, b)
+
+    units = [None] * 16
+    den = [None] * 16
+    for colour in range(3):
+        axis3 = ORDERS[colour][2]
+        lo, hi = UNIT_LO[colour], UNIT_HI[colour]
+        for step in (1, 3, 2):
+            for copy in pending[colour, step]:
+                copy.wait_recv()
+        stats = [s2[colour]] + [q3[colour, i] for i in range(3)]
+        merged, factors = merge_stats(stats, coord[axis3] * HEAD_STRIDE[axis3])
+        for bt in range(lo // 4, (hi - 1) // 4 + 1):
+            fb = [spread(f[bt - colour], 0) for f in factors]
+            dn = spread(merged[bt - colour], 64)
+            for unit in range(max(lo, bt * 4), min(hi, bt * 4 + 4)):
+                total = fb[0] * v2[unit, coord[axis3]]
+                for k in range(3):
+                    total = total + fb[k + 1] * r3[k, unit]
+                units[unit] = total / dn
+    o_lat = jnp.concatenate(
+        [jnp.concatenate([units[bt * 4 + kt] for kt in range(4)], axis=1) for bt in range(4)], axis=0).astype(jnp.bfloat16)
+    o_head = jnp.dot(o_lat, wuv_h[...], preferred_element_type=jnp.float32).astype(jnp.bfloat16)
+    load_out.wait()
+    for half in range(2):
+        for cg in range(4):
+            base = half * 2560 + cg * 640
+            part = jnp.dot(o_head, wout_v[:, base:base + 640], preferred_element_type=jnp.float32)
+            for bt in range(4):
+                y_buf[half, bt, cg] = part[bt * 8:bt * 8 + 8, :]
+
+    pair = send(y_buf.at[1 - tp], y_in, {'tp': 1 - tp})
+    pair.wait_recv()
+    for bt in range(4):
+        for cg in range(4):
+            y_in[bt, cg] = y_in[bt, cg] + y_buf[tp, bt, cg]
+
+    for colour in range(2):
+        cols = pl.ds(OUT_LO[colour], OUT_HI[colour] - OUT_LO[colour])
+        axis = colour
+        for step in (2, 1, 3):
+            pc = peer_coord(axis, step)
+            src = y_in.at[pc, :, :, cols] if axis == 0 else y_in.at[:, pc, :, cols]
+            pending[colour, step] = send(src, t1.at[step - 1, :, :, cols], peer_id(axis, step))
+    for colour in range(2):
+        cols = pl.ds(OUT_LO[colour], OUT_HI[colour] - OUT_LO[colour])
+        axis, axis2 = colour, 1 - colour
+        for step in (1, 3, 2):
+            pending[colour, step].wait_recv()
+        for i in range(4):
+            own = y_in[coord[0], i, :, cols] if axis == 0 else y_in[i, coord[1], :, cols]
+            p1[i, :, cols] = own + t1[0, i, :, cols] + t1[1, i, :, cols] + t1[2, i, :, cols]
+        for step in (2, 1, 3):
+            pending[colour, step] = send(
+                p1.at[peer_coord(axis2, step), :, cols], t2.at[step - 1, :, cols], peer_id(axis2, step))
+    for colour in range(2):
+        cols = pl.ds(OUT_LO[colour], OUT_HI[colour] - OUT_LO[colour])
+        axis2 = 1 - colour
+        for step in (1, 3, 2):
+            pending[colour, step].wait_recv()
+        p2[:, cols] = p1[coord[axis2], :, cols] + t2[0, :, cols] + t2[1, :, cols] + t2[2, :, cols]
+
+    for step in (2, 1, 3):
+        pending[0, step] = send(p2, zbuf.at[coord[2]], peer_id(2, step))
+    zbuf[coord[2]] = p2[...]
+    for step in (1, 3, 2):
+        pending[0, step].wait_recv()
+    g_buf[tp, coord[0], coord[1]] = (zbuf[0] + zbuf[1]) + (zbuf[2] + zbuf[3])
+
+    for colour in range(2):
+        cols = pl.ds(OUT_LO[colour], OUT_HI[colour] - OUT_LO[colour])
+        axis2 = 1 - colour
+        mine = g_buf.at[tp, coord[0], coord[1], :, cols]
+        for step in (2, 1, 3):
+            pending[colour, step] = send(mine, mine, peer_id(axis2, step))
+    for colour in range(2):
+        cols = pl.ds(OUT_LO[colour], OUT_HI[colour] - OUT_LO[colour])
+        axis = colour
+        for step in (1, 3, 2):
+            pending[colour, step].wait_recv()
+        mine = g_buf.at[tp, coord[0], :, :, cols] if axis == 0 else g_buf.at[tp, :, coord[1], :, cols]
+        for step in (2, 1, 3):
+            pending[colour, step] = send(mine, mine, peer_id(axis, step))
+    for colour in range(2):
+        for step in (1, 3, 2):
+            pending[colour, step].wait_recv()
+    pair = send(g_buf.at[tp], g_buf.at[tp], {'tp': 1 - tp})
+    pair.wait_recv()
+    for half in range(2):
+        for cg in range(4):
+            base = half * 2560 + cg * 640
+            full = jnp.concatenate([g_buf[half, bt, cg] for bt in range(4)], axis=0)
+            out_ref[:, base:base + 640] = (hid_ref[:, base:base + 640].astype(jnp.float32) + full).astype(jnp.bfloat16)
+    for copy in started:
+        copy.wait_send()
+
+
+N_SENDS = 54 + 1 + 12 + 3 + 12 + 1
+
+
+def tail(u_parts, stats, hidden, w_uv, w_out):
+    f32, bf16 = jnp.float32, jnp.bfloat16
+    vmem = pl.BlockSpec(memory_space=pltpu.VMEM)
+    hbm = pl.BlockSpec(memory_space=pl.ANY)
+    return pl.pallas_call(
+        tail_kernel,
+        out_shape=jax.ShapeDtypeStruct((32, 5120), bf16),
+        in_specs=[vmem, vmem, vmem, hbm, hbm],
+        out_specs=vmem,
+        scratch_shapes=[
+            pltpu.VMEM((3, 16, 4, 4, 8, 128), f32),
+            pltpu.VMEM((16, 4, 4, 8, 128), f32),
+            pltpu.VMEM((3, 16, 4, 8, 128), f32),
+            pltpu.VMEM((16, 4, 8, 128), f32),
+            pltpu.VMEM((3, 16, 8, 128), f32),
+            pltpu.VMEM((3, 2, 8, 128), f32),
+            pltpu.VMEM((3, 2, 8, 128), f32),
+            pltpu.VMEM((3, 3, 2, 8, 128), f32),
+            pltpu.VMEM((3, 3, 2, 8, 128), f32),
+            pltpu.VMEM((3, 3, 2, 8, 128), f32),
+            pltpu.VMEM((512, 8, 128), bf16),
+            pltpu.VMEM((512, 128), bf16),
+            pltpu.VMEM((128, 5120), bf16),
+            pltpu.VMEM((2, 4, 4, 8, 640), f32),
+            pltpu.VMEM((4, 4, 8, 640), f32),
+            pltpu.VMEM((3, 4, 8, 640), f32),
+            pltpu.VMEM((3, 8, 640), f32),
+            pltpu.VMEM((4, 8, 640), f32),
+            pltpu.VMEM((8, 640), f32),
+            pltpu.VMEM((4, 8, 640), f32),
+            pltpu.VMEM((2, 4, 4, 8, 640), f32),
+            pltpu.SemaphoreType.DMA((N_SENDS,)),
+            pltpu.SemaphoreType.DMA((N_SENDS,)),
+            pltpu.SemaphoreType.DMA((2,)),
+        ],
+        compiler_params=pltpu.CompilerParams(collective_id=0, has_side_effects=True),
+        name='tail',
+    )(u_parts, stats, hidden, w_uv, w_out)
+
+
 def solution(mesh):
     row_spec = P('dp', None)
     cache_spec = P('dp', 'sp', None)
@@ -53,7 +336,6 @@
     out_specs = (row_spec, cache_spec, cache_spec)
 
     def local_step(hidden, lat_cache, rope_cache, positions, w_dq, gain_q, w_dkv, gain_kv, w_uq, w_uk, w_uv, w_out):
-        rows_local = hidden.shape[0]
         seq_local = lat_cache.shape[1]
         score_scale = YARN_MSCALE ** 2 / math.sqrt(w_uq.shape[2])
         q_abs, q_rope, lat_new, rope_new = project_inputs(hidden, positions, w_dq, gain_q, w_dkv, gain_kv, w_uq, w_uk)
@@ -64,14 +346,13 @@
         scores = (jnp.einsum('bhk,bsk->bhs', q_abs, lat_all, preferred_element_type=jnp.float32) + jnp.einsum('bhr,bsr->bhs', q_rope, rope_all, preferred_element_type=jnp.float32)) * score_scale
         key_valid = slot_ids[None, None, :] <= positions[:, None, None]
         scores = jnp.where(key_valid, scores, MASK_VALUE)
-        max_global = lax.pmax(jnp.max(scores, axis=-1), 'sp')
-        weights = jnp.exp(scores - max_global[:, :, None])
+        max_local = jnp.max(scores, axis=-1)
+        weights = jnp.exp(scores - max_local[:, :, None])
         lat_part = jnp.einsum('bhs,bsk->bhk', weights.astype(jnp.bfloat16), lat_all, preferred_element_type=jnp.float32)
-        denominator, lat_sum = lax.psum((jnp.sum(weights, axis=-1), lat_part), 'sp')
-        o_lat = (lat_sum / denominator[:, :, None]).astype(jnp.bfloat16)
-        o_heads = jnp.einsum('bhk,khv->bhv', o_lat, w_uv, preferred_element_type=jnp.float32).astype(jnp.bfloat16)
-        attn_part = jnp.dot(o_heads.reshape(rows_local, -1), w_out, preferred_element_type=jnp.float32)
-        attn_out = lax.psum(attn_part, 'tp')
-        return (hidden.astype(jnp.float32) + attn_out).astype(jnp.bfloat16), lat_all, rope_all
+        den_local = jnp.sum(weights, axis=-1)
+        stats = jnp.concatenate([max_local, den_local], axis=1).reshape(4, 8, 128)
+        u_parts = lat_part.reshape(4, 8, 64, 4, 128).transpose(0, 3, 2, 1, 4).reshape(16, 4, 4, 4, 8, 128)
+        out = tail(u_parts, stats, hidden, w_uv, w_out)
+        return out, lat_all, rope_all
 
     return jax.shard_map(local_step, mesh=mesh, in_specs=in_specs, out_specs=out_specs, check_vma=False)

time: 859 us -> 145 us (0.17)
  blocking collectives: 584 us -> 0 us
  waiting for transfers between devices: 128 us -> 0 us
  Pallas kernels: 0 us -> 64.7 us
  matrix products: 118 us -> 58.6 us
  between operations: 14.5 us -> 0.83 us
  local copies, waits for them, and re-layouts: 2.15 us -> 13.6 us
    pmax x1 -> x0, blocking collectives: 296 us -> none  [local_step(): max_global = lax.pmax(jnp.max(scores, axis=-1), 'sp')]
    psum x1 -> x0, blocking collectives: 287 us -> none  [local_step(): denominator, lat_sum = lax.psum((jnp.sum(weights, axis=-1), lat_part), 'sp')]
    psum x2 -> x0, waiting for transfers between devices: 127 us -> none  [the longest x1 127 us: local_step(): attn_out = lax.psum(attn_part, 'tp')]
    pallas_call x0 -> x1, Pallas kernels: none -> 64.7 us  [tail(): pl.pallas_call(tail_kernel, out_shape=jax.ShapeDtypeStruct((32, 5120), bf...]
    dot_general x2 -> x0, matrix products: 51.6 us -> none  [the longest x1 29.7 us: local_step(): jnp.dot(o_heads.reshape(rows_local, -1), w_out, preferred_element_type=jn...]
    reshape x0 -> x2, local copies, waits for them, and re-layouts: none -> 11.8 us  [local_step(): lat_part.reshape(4, 8, 64, 4, 128).transpose(0, 3, 2, 1, 4)]
  transfers between devices with their start and end apart: 2 -> 0, of which waited for: 1 -> 0; matrix products, arithmetic and copies ran while one was open for 0% -> 0% of each run, Pallas kernels for 0% -> 0%
where the time goes in v1:
time: 145 us
  Pallas kernels  64.7 us (45%)
  matrix products  58.6 us (40%)
  local copies, waits for them, and re-layouts  13.6 us (9%)
  other arithmetic  7.18 us (5%)
    pallas_call x1, Pallas kernels, tail(): pl.pallas_call(tail_kernel, out_shape=jax.ShapeDtypeStruct((32, 5120), bf...  64.7 us
    dot_general x1, matrix products, project_inputs(): jnp.einsum('bhn,khn->bhk', q_full[:, :, :nope_dim], w_uk, preferred_eleme...  21.2 us
    dot_general x1, matrix products, project_inputs(): jnp.einsum('br,rhd->bhd', c_q, w_uq, preferred_element_type=jnp.float32)  17.9 us
    reshape x2, local copies, waits for them, and re-layouts, local_step(): lat_part.reshape(4, 8, 64, 4, 128).transpose(0, 3, 2, 1, 4)  11.8 us
    dot_general x1, matrix products, project_inputs(): jnp.dot(hidden, w_dq, preferred_element_type=jnp.float32)  8.27 us
    dot_general x1, matrix products, project_inputs(): jnp.dot(hidden, w_dkv, preferred_element_type=jnp.float32)  4.59 us
    dot_general x1, matrix products, local_step(): jnp.einsum('bhs,bsk->bhk', weights.astype(jnp.bfloat16), lat_all, preferr...  3.46 us

profile of v1, /device:TPU:1, one launch (start us, length us, event | category | flops | bytes accessed | tf_op | source)
XLA Modules:
  0.0 144.9 jit_solution(17522611403011179417)
XLA Ops:
  0.6 0.0 copy-start.2
  0.6 0.7 convert_element_type.70
  1.4 0.7 convert_element_type.67
  2.0 0.7 convert_element_type.60
  2.7 0.7 broadcast_compare_fusion.1
  3.5 4.6 %convolution_convert_fusion.2 = bf16[32,576]{1,0:T(8,128)(2,1)S(1)} fusion(bf16[32,5120]{1,0:T(8,128)(2,1)} %hid_ref.1, bf16[5120,576]{0,1:T(8,128)(2,1)} %param.18), kind=kOutput, calls=%fused_computation.13 | convolution fusion | flops 188762112 | bytes 6262784 | tf_op jit(solution)/shard_map/dot_general | solution.py:53
  8.1 0.1 fusion.17
  8.2 0.1 fusion.19
  8.3 0.1 multiply_cosine_fusion
  8.4 0.1 pad_maximum_fusion.1
  8.5 8.3 %multiply_reduce_fusion = (f32[32]{0:T(128)S(1)}, f32[32,1536]{1,0:T(8,128)S(1)}) fusion(bf16[32,5120]{1,0:T(8,128)(2,1)S(1)} %copy-done.2, bf16[5120,1536]{1,0:T(8,128)(2,1)} %param.16), kind=kOutput, calls=%fused_computation.24 | convolution fusion | flops 503513056 | bytes 16253056 | tf_op jit(solution)/shard_map/dot_general | solution.py:48
  16.8 0.0 copy-start.3
  16.8 17.9 %convolution_convert_fusion.1 = bf16[32,64,192]{2,0,1:T(8,128)(2,1)S(1)} fusion(bf16[1536,64,192]{0,2,1:T(8,128)(2,1)} %param.20, f32[32,1536]{1,0:T(8,128)S(1)} %get-tuple-element.14, f32[1536]{0:T(1024)S(1)} %convert_element_type.60, f32[32]{0:T(128)S(1)} %add_rsqrt_fusion.1), kind=kOutput, calls=%fused_computation.12 | convolution fusion | flops 1208500224 | bytes 38738048 | tf_op jit(solution)/shard_map/br,rhd->bhd/dot_general | solution.py:50
  34.7 0.3 broadcast_select_fusion.1
  35.0 0.0 copy-start.1
  35.0 0.1 slice_convert_fusion
  35.1 0.0 slice-start
  35.2 0.4 subtract_convert_fusion
  35.6 0.3 pad_maximum_fusion
  35.9 0.0 slice-start.1
  35.9 21.2 %fusion = bf16[64,32,512]{2,1,0:T(8,128)(2,1)S(1)} fusion(bf16[512,64,128]{2,1,0:T(8,128)(2,1)} %param.21, bf16[32,64,192]{2,0,1:T(8,128)(2,1)S(1)} %convolution_convert_fusion.1), kind=kOutput, calls=%fused_computation | convolution fusion | flops 268435456 | bytes 11010048 | tf_op jit(solution)/shard_map/bhn,khn->bhk/dot_general | solution.py:52
  57.1 1.4 broadcast_select_fusion
  58.5 0.0 copy-start
  58.5 2.6 %fusion.4 = f32[32,64,256]{2,1,0:T(8,128)S(1)} fusion(bf16[32,256,512]{2,1,0:T(8,128)(2,1)S(1)} %broadcast_select_fusion, bf16[64,32,512]{2,1,0:T(8,128)(2,1)S(1)} %fusion), kind=kOutput, calls=%fused_computation.7 | convolution fusion | flops 536870912 | bytes 12582912 | tf_op jit(solution)/shard_map/bhk,bsk->bhs/dot_general | solution.py:346
  61.1 0.7 fusion.20
  61.8 0.7 fusion.6
  62.5 0.7 maximum_bitcast_fusion.st_ref
  63.2 3.5 %fusion.8 = f32[32,64,512]{2,1,0:T(8,128)} fusion(bf16[32,256,512]{2,1,0:T(8,128)(2,1)S(1)} %broadcast_select_fusion, f32[32,64,256]{2,1,0:T(8,128)S(1)} %get-tuple-element.16, f32[32,64]{1,0:T(8,128)S(1)} %get-tuple-element.15), kind=kOutput, calls=%fused_computation.14 | convolution fusion | flops 537919488 | bytes 14688256 | tf_op jit(solution)/shard_map/bhs,bsk->bhk/dot_general | solution.py:351
  66.6 5.2 %reshape.167 = f32[4,8,64,4,128]{4,3,2,1,0:T(4,128)} reshape(f32[32,64,512]{2,1,0:T(8,128)} %fusion.8) | data formatting | bytes 8388608 | tf_op jit(solution)/shard_map/reshape | solution.py:354
  71.9 6.6 %copy.16 = f32[4,8,64,4,128]{4,1,2,3,0:T(8,128)} copy(f32[4,8,64,4,128]{4,3,2,1,0:T(4,128)} %reshape.167) | data formatting | bytes 8388608 | tf_op jit(solution)/shard_map/reshape | solution.py:354
  78.4 64.7 %tail.1 = bf16[32,5120]{1,0:T(8,128)(2,1)} custom-call(f32[16,4,4,4,8,128]{5,4,3,2,1,0:T(8,128)} %bitcast.19, f32[4,8,128]{2,1,0:T(8,128)} %maximum_bitcast_fusion.st_ref, bf16[32,5120]{1,0:T(8,128)(2,1)} %hid_ref.1, bf16[512,64,128]{2,1,0:T(8,128)(2,1)} %wuv_ref.1, bf16[8192,5120]{1,0:T(8,128)(2,1)} %wout_ref.1), custom_call_target="tpu_custom_call" | custom-call | tf_op jit(solution)/shard_map/tail/pallas_call | solution.py:295
  143.2 1.7 %copy.30 = bf16[32,5120]{1,0:T(8,128)(2,1)} copy(bf16[32,5120]{1,0:T(8,128)(2,1)} %tail.1) | data formatting | bytes 655360
  (12 shorter events, 0.0 us)
Async XLA Ops:
  0.6 7.9 %copy-start.2 = (bf16[32,5120]{1,0:T(8,128)(2,1)S(1)}, bf16[32,5120]{1,0:T(8,128)(2,1)}, u32[]{:S(2)}) copy-start(bf16[32,5120]{1,0:T(8,128)(2,1)} %hid_ref.1) | copy-start | bytes 983044
  16.8 17.9 %copy-start.3 = (bf16[32,256,64]{1,2,0:T(8,128)(2,1)S(1)}, bf16[32,256,64]{1,2,0:T(8,128)(2,1)}, u32[]{:S(2)}) copy-start(bf16[32,256,64]{1,2,0:T(8,128)(2,1)} %param.14) | copy-start | bytes 3145732
  35.0 26.1 %copy-start.1 = (bf16[32,256,64]{1,2,0:T(8,128)(2,1)}, bf16[32,256,64]{1,2,0:T(8,128)(2,1)S(1)}, u32[]{:S(2)}) copy-start(bf16[32,256,64]{1,2,0:T(8,128)(2,1)S(1)} %broadcast_select_fusion.1) | copy-start | bytes 3145732
  35.1 21.9 %slice-start = ((s8[8388608]{0:T(1024)(128)(4,1)}), s8[4194304]{0:T(1024)(128)(4,1)S(1)}, s32[]{:S(2)}) async-start(s8[8388608]{0:T(1024)(128)(4,1)} %bitcast.20), calls=%async_computation | async-start | bytes 8388608
  35.9 21.2 %slice-start.1 = ((s8[8388608]{0:T(1024)(128)(4,1)}), s8[4194304]{0:T(1024)(128)(4,1)S(1)}, s32[]{:S(2)}) async-start(s8[8388608]{0:T(1024)(128)(4,1)} %bitcast.20), calls=%async_computation.1 | async-start | bytes 8388608
  58.5 4.6 %copy-start = (bf16[32,256,512]{2,1,0:T(8,128)(2,1)}, bf16[32,256,512]{2,1,0:T(8,128)(2,1)S(1)}, u32[]{:S(2)}) copy-start(bf16[32,256,512]{2,1,0:T(8,128)(2,1)S(1)} %broadcast_select_fusion) | copy-start | bytes 25165828
